TPU v7x, 32 devices: a whole 2x2x4 slice. The times are simulated.
32 devices in a mesh: head: 2 (over core), seq: 8 (over z, y), mp: 2 (over x).
Axes of the slice: x: 2, y: 2, z: 4, core: 2. Of those that a mesh axis runs over, the one named last changes fastest.
Arguments:
- trunk: bfloat16 [128, 8192], P('seq', 'mp'), may hold values from -6 to 6
- branch: bfloat16 [2, 128, 8192], P('head', 'seq', 'mp'), may hold values from -6 to 6
- unembed: bfloat16 [18432, 8192], P('seq', 'mp'), may hold values from -0.09375 to 0.09375
- targets: int32 [2, 128], P('head'), may hold values from 0 to 18431
- loss_grad: float32 [2, 128], P('head'), may hold values from 0.25 to 4
Outputs:
- d_branch: bfloat16 [2, 128, 8192], P('head', 'seq', 'mp')
- d_trunk: bfloat16 [128, 8192], P('seq', 'mp')
- d_unembed: float32 [18432, 8192], P('seq', 'mp')
All inputs are finite; a program needn't handle non-finite values.
Results may differ from a plain program's by a relative error of at most 0.0051.
Values may be sent and summed in bfloat16 or wider, within the bound.
No kernel may reach another device: no remote copies, remote signals or barrier semaphores. Data moves between devices by JAX's collectives and lax.ppermute only.
A program may use at most 192 MiB of HBM per device.

v0:
```python
import jax
import jax.numpy as jnp
from jax import lax
from jax.sharding import PartitionSpec as P

soft_cap = 30.0


def shards(trunk, branch, unembed, targets, loss_grad):
    block_rows = unembed.shape[0]
    hidden = (trunk.astype(jnp.float32) + branch[0].astype(jnp.float32)).astype(jnp.bfloat16)
    gathered = lax.all_gather(hidden, "seq", axis=0, tiled=True)
    seq_index = lax.axis_index("seq")
    scores = lax.psum(
        lax.dot_general(
            unembed, gathered, (((1,), (1,)), ((), ())), preferred_element_type=jnp.float32
        ),
        "mp",
    )
    first_vocab = seq_index * block_rows
    squashed = jnp.tanh(scores / soft_cap)
    exponent = jnp.exp(soft_cap * squashed)
    totals = lax.psum(jnp.sum(exponent, axis=0), "seq")
    vocab_ids = first_vocab + lax.iota(jnp.int32, scores.shape[0])
    onehot = (vocab_ids[:, None] == targets[0][None, :]).astype(jnp.float32)
    slope = (
        loss_grad[0][None, :] * (exponent / totals[None, :] - onehot) * (1.0 - squashed * squashed)
    )
    grad_logits = slope.astype(jnp.bfloat16)
    weight_grad = jnp.dot(grad_logits, gathered, preferred_element_type=jnp.float32)
    row_grad = lax.psum_scatter(
        lax.dot_general(
            grad_logits, unembed, (((0,), (0,)), ((), ())), preferred_element_type=jnp.float32
        ),
        "seq",
        scatter_dimension=0,
        tiled=True,
    )
    trunk_sum, unembed_sum = lax.psum((row_grad, weight_grad), "head")
    return (row_grad.astype(jnp.bfloat16)[None], trunk_sum.astype(jnp.bfloat16), unembed_sum)


def solution(mesh):
    in_specs = (
        P("seq", "mp"),
        P("head", "seq", "mp"),
        P("seq", "mp"),
        P("head", None),
        P("head", None),
    )
    out_specs = (P("head", "seq", "mp"), P("seq", "mp"), P("seq", "mp"))
    return jax.shard_map(shards, mesh=mesh, in_specs=in_specs, out_specs=out_specs, check_vma=False)
```

profile of v0, /device:TPU:0, one launch (start us, length us, event | category | flops | bytes accessed | tf_op | source)
XLA Modules:
  0.0 359.2 jit_solution(3892800967753359351)
XLA Ops:
  7.2 0.0 all-gather.2.cloned.1.call-start
  7.2 1.7 fusion.1
  8.9 0.0 all-gather.2.cloned.1.call-update
  8.9 0.0 all-reduce.4.cloned.1.call-start
  8.9 44.8 %all-gather.2.cloned.1.call-done = bf16[128,4096]{1,0:T(8,128)(2,1)} async-done(((bf16[16,4096]{1,0:T(8,128)(2,1)}), bf16[128,4096]{1,0:T(8,128)(2,1)}) %all-gather.2.cloned.1.call-update) | async-done | bytes 1048592 | tf_op jit(solution)/shard_map/all_gather | solution.py:12
  53.7 14.0 %convolution_bitcast_fusion = f32[2304,128]{0,1:T(8,128)} fusion(bf16[128,4096]{1,0:T(8,128)(2,1)} %all-gather.2.cloned.1.call-done, bf16[2304,4096]{1,0:T(8,128)(2,1)} %param.7), kind=kOutput, calls=%fused_computation | convolution fusion | flops 2415919104 | bytes 21102592 | tf_op jit(solution)/shard_map/dot_general | solution.py:15
  67.8 0.0 copy-start.2
  67.8 0.0 copy-start.3
  67.8 0.0 all-reduce.4.cloned.1.call-update
  67.8 0.0 reduce-scatter.2.cloned.1.call-start
  67.9 41.8 %all-reduce.4.cloned.1.call-done = f32[2304,128]{0,1:T(8,128)} async-done(((f32[2304,128]{0,1:T(8,128)}), f32[2304,128]{0,1:T(8,128)}) %all-reduce.4.cloned.1.call-update) | async-done | bytes 1179664 | tf_op jit(solution)/shard_map/psum | solution.py:14
  109.6 0.0 copy-start
  109.6 1.8 fusion
  111.4 21.4 %psum.29 = f32[128]{0:T(128)S(1)} all-reduce(f32[128]{0:T(128)S(1)} %fusion), channel_id=1, replica_groups=mesh['head'=2,'seq'=8,'mp'=2] {'seq'}, use_global_device_ids=true, to_apply=%region_2.0 | all-reduce | flops 128 | bytes 1024 | tf_op jit(solution)/shard_map/psum | solution.py:23
  132.7 0.0 copy-done.2
  132.7 0.0 copy-done.3
  132.7 0.0 copy-done
  132.7 10.8 %fusion.3 = f32[128,4096]{1,0:T(8,128)} fusion(bf16[2304,4096]{1,0:T(8,128)(2,1)} %param.7, f32[2304,128]{0,1:T(8,128)S(1)} %copy-done, s32[2304]{0:T(1024)S(1)} %iota_add_fusion, f32[128]{0:T(128)S(1)} %psum.29, f32[128]{0:T(128)S(1)} %bitcast.13, s32[128]{0:T(128)S(1)} %bitcast.15), kind=kOutput, calls=%fused_computation.10 | convolution fusion | flops 2419163136 | bytes 22161920 | tf_op jit(solution)/shard_map/dot_general | solution.py:32
  143.5 0.0 copy-start.1
  143.5 0.0 reduce-scatter.2.cloned.1.call-update
  143.6 0.0 all-reduce.6.cloned.1.call-start
  143.6 1.1 copy-done.1
  144.8 15.9 %fusion.2 = f32[2304,4096]{1,0:T(8,128)} fusion(bf16[128,4096]{1,0:T(8,128)(2,1)S(1)} %copy-done.1, f32[2304,128]{0,1:T(8,128)S(1)} %copy-done, s32[2304]{0:T(1024)S(1)} %iota_add_fusion, f32[128]{0:T(128)S(1)} %psum.29, f32[128]{0:T(128)S(1)} %bitcast.14, s32[128]{0:T(128)S(1)} %bitcast.16), kind=kOutput, calls=%fused_computation.9 | convolution fusion | flops 2419163136 | bytes 39987712 | tf_op jit(solution)/shard_map/dot_general | solution.py:30
  160.6 0.0 all-reduce.6.cloned.1.call-update
  160.7 47.7 %reduce-scatter.2.cloned.1.call-done = f32[16,4096]{1,0:T(8,128)} async-done(((f32[128,4096]{1,0:T(8,128)}), f32[16,4096]{1,0:T(8,128)}) %reduce-scatter.2.cloned.1.call-update) | async-done | bytes 262160 | tf_op jit(solution)/shard_map/reduce_scatter | solution.py:31
  208.4 1.6 convert_bitcast_fusion
  210.0 5.4 %all-reduce.7 = bf16[16,4096]{1,0:T(8,128)(2,1)} all-reduce(f32[16,4096]{1,0:T(8,128)} %reduce-scatter.2.cloned.1.call-done), channel_id=1, replica_groups=mesh['head'=2,'seq'=8,'mp'=2] {'head'}, use_global_device_ids=true, to_apply=%region_4.0 | all-reduce | flops 65536 | bytes 393216 | tf_op jit(solution)/shard_map/psum | solution.py:39
  215.4 110.0 %all-reduce.6.cloned.1.call-done = f32[2304,4096]{1,0:T(8,128)} async-done(((f32[2304,4096]{1,0:T(8,128)}), f32[2304,4096]{1,0:T(8,128)}) %all-reduce.6.cloned.1.call-update) | async-done | bytes 37748752 | tf_op jit(solution)/shard_map/psum | solution.py:39
  325.4 27.3 %copy.12 = f32[2304,4096]{1,0:T(8,128)} copy(f32[2304,4096]{1,0:T(8,128)} %all-reduce.6.cloned.1.call-done) | data formatting | bytes 75497472
  (1 shorter events, 0.0 us)
Async XLA Ops:
  7.2 46.5 %all-gather.2.cloned.1.call-start = ((), (), s32[]{:S(2)}) async-start(), calls=%async_computation.1 | async-start | bytes 1179648 | tf_op jit(solution)/shard_map/all_gather | solution.py:12
  8.9 100.7 %all-reduce.4.cloned.1.call-start = ((), (), s32[]{:S(2)}) async-start(), calls=%async_computation.2 | async-start | bytes 2359296 | tf_op jit(solution)/shard_map/psum | solution.py:14
  67.8 65.0 %copy-start.2 = (f32[1,128]{1,0:T(1,128)S(1)}, f32[1,128]{1,0:T(1,128)}, u32[]{:S(2)}) copy-start(f32[1,128]{1,0:T(1,128)} %param.9) | copy-start | bytes 1540
  67.8 65.0 %copy-start.3 = (s32[1,128]{1,0:T(1,128)S(1)}, s32[1,128]{1,0:T(1,128)}, u32[]{:S(2)}) copy-start(s32[1,128]{1,0:T(1,128)} %param.8) | copy-start | bytes 1540
  67.8 140.6 %reduce-scatter.2.cloned.1.call-start = ((), (), s32[]{:S(2)}) async-start(), calls=%async_computation.3 | async-start | bytes 2359296 | tf_op jit(solution)/shard_map/reduce_scatter | solution.py:31
  109.6 23.1 %copy-start = (f32[2304,128]{0,1:T(8,128)S(1)}, f32[2304,128]{0,1:T(8,128)}, u32[]{:S(2)}) copy-start(f32[2304,128]{0,1:T(8,128)} %all-reduce.4.cloned.1.call-done) | copy-start | bytes 3538948
  143.5 1.2 copy-start.1
  143.6 181.8 %all-reduce.6.cloned.1.call-start = ((), (), s32[]{:S(2)}) async-start(), calls=%async_computation.4 | async-start | bytes 75497472 | tf_op jit(solution)/shard_map/psum | solution.py:39
Sparse Core Ops, SparseCore 0:
  10.7 42.9 all-gather.1
  67.9 41.6 all-reduce.3
  143.7 64.6 reduce-scatter.1
  211.3 114.0 all-reduce.5
where the time goes:
time: 360 us; the launch traced here: 359 us
  waiting for transfers between devices  244 us (68%)
  matrix products  40.7 us (11%)
  local copies, waits for them, and re-layouts  28.4 us (8%)
  blocking collectives  26.8 us (7%)
  between operations  13.8 us (4%)
  other arithmetic  5.04 us (1%)
    psum x1, waiting for transfers between devices, shards(): trunk_sum, unembed_sum = lax.psum((row_grad, weight_grad), 'head')  110 us
    reduce_scatter x1, waiting for transfers between devices, shards(): lax.psum_scatter(lax.dot_general(grad_logits, unembed, (((0,), (0,)), (()...  47.7 us
    all_gather x1, waiting for transfers between devices, shards(): gathered = lax.all_gather(hidden, 'seq', axis=0, tiled=True)  44.8 us
    psum x1, waiting for transfers between devices, shards(): lax.psum(lax.dot_general(unembed, gathered, (((1,), (1,)), ((), ())), pre...  41.8 us
    unnamed x9, local copies, waits for them, and re-layouts  28.4 us
    psum x1, blocking collectives, shards(): totals = lax.psum(jnp.sum(exponent, axis=0), 'seq')  21.4 us
    dot_general x1, matrix products, shards(): jnp.dot(grad_logits, gathered, preferred_element_type=jnp.float32)  15.9 us
    dot_general x1, matrix products, shards(): lax.dot_general(unembed, gathered, (((1,), (1,)), ((), ())), preferred_el...  14 us
  transfers between devices with their start and end apart: 4, of which 4 were waited for; matrix products, arithmetic and copies ran while one was open for 5% of the time, Pallas kernels for 0%

commit v1 on v0

--- a/solution.py
+++ b/solution.py
@@ -9,7 +9,14 @@
 def shards(trunk, branch, unembed, targets, loss_grad):
     block_rows = unembed.shape[0]
     hidden = (trunk.astype(jnp.float32) + branch[0].astype(jnp.float32)).astype(jnp.bfloat16)
-    gathered = lax.all_gather(hidden, "seq", axis=0, tiled=True)
+    ways, here, hop = (lax.axis_size("seq"), lax.axis_index("seq"), hidden.shape[0])
+    line, have = (hidden, 1)
+    while have < ways:
+        line = jnp.concatenate(
+            [line, lax.ppermute(line, "seq", [(d, (d - have) % ways) for d in range(ways)])], axis=0
+        )
+        have = 2 * have
+    gathered = jnp.roll(line, here * hop, axis=0)
     seq_index = lax.axis_index("seq")
     scores = lax.psum(
         lax.dot_general(

time: 360 us -> 358 us (level)
  starting transfers between devices: 0.16 us -> 8.36 us
  waiting for transfers between devices: 244 us -> 236 us
    all_gather x1 -> x0, waiting for transfers between devices: 44.8 us -> none  [shards(): gathered = lax.all_gather(hidden, 'seq', axis=0, tiled=True)]
    ppermute x0 -> x3, waiting for transfers between devices: none -> 32 us  [shards(): lax.ppermute(line, 'seq', [(d, (d - have) % ways) for d in range(ways)])]
    ppermute x0 -> x3, starting transfers between devices: none -> 8.24 us  [shards(): lax.ppermute(line, 'seq', [(d, (d - have) % ways) for d in range(ways)])]
    unnamed x9 -> x13, local copies, waits for them, and re-layouts: 28.4 us -> 27.4 us
  transfers between devices with their start and end apart: 4 -> 6, of which waited for: 4 -> 6; matrix products, arithmetic and copies ran while one was open for 5% -> 5% of each run, Pallas kernels for 0% -> 0%
where the time goes in v1:
time: 358 us; the launch traced here: 357 us
  waiting for transfers between devices  236 us (66%)
  matrix products  40.6 us (11%)
  local copies, waits for them, and re-layouts  27.4 us (8%)
  blocking collectives  26.8 us (7%)
  between operations  13.8 us (4%)
  starting transfers between devices  8.36 us (2%)
  other arithmetic  4.44 us (1%)
    psum x1, waiting for transfers between devices, shards(): trunk_sum, unembed_sum = lax.psum((row_grad, weight_grad), 'head')  110 us
    reduce_scatter x1, waiting for transfers between devices, shards(): lax.psum_scatter(lax.dot_general(grad_logits, unembed, (((0,), (0,)), (()...  48.6 us
    psum x1, waiting for transfers between devices, shards(): lax.psum(lax.dot_general(unembed, gathered, (((1,), (1,)), ((), ())), pre...  45 us
    ppermute x3, waiting for transfers between devices, shards(): lax.ppermute(line, 'seq', [(d, (d - have) % ways) for d in range(ways)])  32 us
    unnamed x13, local copies, waits for them, and re-layouts  27.4 us
    psum x1, blocking collectives, shards(): totals = lax.psum(jnp.sum(exponent, axis=0), 'seq')  21.4 us
    dot_general x1, matrix products, shards(): jnp.dot(grad_logits, gathered, preferred_element_type=jnp.float32)  16.1 us
    dot_general x1, matrix products, shards(): lax.dot_general(unembed, gathered, (((1,), (1,)), ((), ())), preferred_el...  13.7 us
  transfers between devices with their start and end apart: 6, of which 6 were waited for; matrix products, arithmetic and copies ran while one was open for 5% of the time, Pallas kernels for 0%

profile of v1, /device:TPU:0, one launch (start us, length us, event | category | flops | bytes accessed | tf_op | source)
XLA Modules:
  0.0 357.1 jit_solution(2494538091465745470)
XLA Ops:
  7.2 0.0 all-reduce.4.cloned.1.call-start
  7.2 1.0 constant_dynamic-update-slice_fusion.7
  8.2 6.1 %collective-permute-start = (bf16[16,4096]{1,0:T(8,128)(2,1)S(1)}, bf16[16,4096]{1,0:T(8,128)(2,1)S(1)}, u32[]{:S(2)}, u32[]{:S(2)}) collective-permute-start(bf16[16,4096]{1,0:T(8,128)(2,1)S(1)} %get-tuple-element.4), channel_id=1, source_target_pairs={{0,14},{2,0},{4,2},{6,4},{8,6},{10,8},{12,10},{14,12},{1,15},{3,1}... | collective-permute-start | bytes 393224 | tf_op jit(solution)/shard_map/ppermute | solution.py:16
  14.3 2.8 collective-permute-done
  17.1 1.6 collective-permute-start.1
  18.7 5.7 %collective-permute-done.1 = bf16[32,4096]{1,0:T(8,128)(2,1)S(1)} collective-permute-done((bf16[32,4096]{1,0:T(8,128)(2,1)S(1)}, bf16[32,4096]{1,0:T(8,128)(2,1)S(1)}, u32[]{:S(2)}, u32[]{:S(2)}) %collective-permute-start.1) | collective-permute-done | bytes 262176 | tf_op jit(solution)/shard_map/ppermute | solution.py:16
  24.4 0.6 collective-permute-start.2
  25.0 23.5 %collective-permute-done.2 = bf16[64,4096]{1,0:T(8,128)(2,1)S(1)} collective-permute-done((bf16[64,4096]{1,0:T(8,128)(2,1)S(1)}, bf16[64,4096]{1,0:T(8,128)(2,1)S(1)}, u32[]{:S(2)}, u32[]{:S(2)}) %collective-permute-start.2) | collective-permute-done | bytes 524320 | tf_op jit(solution)/shard_map/ppermute | solution.py:16
  48.7 13.7 %convolution_bitcast_fusion = f32[2304,128]{0,1:T(8,128)} fusion(bf16[2304,4096]{1,0:T(8,128)(2,1)} %param.7, bf16[256,4096]{1,0:T(8,128)(2,1)S(1)} %constant_dynamic-update-slice_fusion, s32[]{:T(128)S(6)} %select_n.14), kind=kOutput, calls=%fused_computation | convolution fusion | flops 2415919104 | bytes 21102596 | tf_op jit(solution)/shard_map/dot_general | solution.py:22
  62.4 0.0 copy-start.1
  62.4 0.0 copy-start.2
  62.4 0.0 all-reduce.4.cloned.1.call-update
  62.4 0.0 reduce-scatter.2.cloned.1.call-start
  62.5 45.0 %all-reduce.4.cloned.1.call-done = f32[2304,128]{0,1:T(8,128)} async-done(((f32[2304,128]{0,1:T(8,128)}), f32[2304,128]{0,1:T(8,128)}) %all-reduce.4.cloned.1.call-update) | async-done | bytes 1179664 | tf_op jit(solution)/shard_map/psum | solution.py:21
  107.5 0.0 copy-start
  107.5 1.8 fusion
  109.2 21.4 %psum.29 = f32[128]{0:T(128)S(1)} all-reduce(f32[128]{0:T(128)S(1)} %fusion), channel_id=1, replica_groups=mesh['head'=2,'seq'=8,'mp'=2] {'seq'}, use_global_device_ids=true, to_apply=%region_2.3 | all-reduce | flops 128 | bytes 1024 | tf_op jit(solution)/shard_map/psum | solution.py:30
  130.6 0.0 copy-done.1
  130.6 0.0 copy-done.2
  130.6 0.0 copy-done
  130.6 10.8 %fusion.7 = f32[128,4096]{1,0:T(8,128)} fusion(bf16[2304,4096]{1,0:T(8,128)(2,1)} %param.7, f32[2304,128]{0,1:T(8,128)S(1)} %copy-done, s32[2304]{0:T(1024)S(1)} %iota_add_fusion, f32[128]{0:T(128)S(1)} %psum.29, f32[128]{0:T(128)S(1)} %bitcast.12, s32[128]{0:T(128)S(1)} %bitcast.14), kind=kOutput, calls=%fused_computation.24 | convolution fusion | flops 2419163136 | bytes 22161920 | tf_op jit(solution)/shard_map/dot_general | solution.py:39
  141.4 0.0 reduce-scatter.2.cloned.1.call-update
  141.4 0.0 all-reduce.6.cloned.1.call-start
  141.5 16.1 %fusion.1 = f32[2304,4096]{1,0:T(8,128)} fusion(bf16[256,4096]{1,0:T(8,128)(2,1)S(1)} %constant_dynamic-update-slice_fusion, s32[]{:T(128)S(6)} %select_n.14, f32[2304,128]{0,1:T(8,128)S(1)} %copy-done, s32[2304]{0:T(1024)S(1)} %iota_add_fusion, f32[128]{0:T(128)S(1)} %psum.29, f32[128]{0:T(128)S(1)} %bitcast.13, s32[128]{0:T(128)S(1)} %bitcast.15), kind=kOutput, calls=%fused_computation.5 | convolution fusion | flops 2419163136 | bytes 39990788 | tf_op jit(solution)/shard_map/dot_general | solution.py:37
  157.5 0.0 all-reduce.6.cloned.1.call-update
  157.6 48.6 %reduce-scatter.2.cloned.1.call-done = f32[16,4096]{1,0:T(8,128)} async-done(((f32[128,4096]{1,0:T(8,128)}), f32[16,4096]{1,0:T(8,128)}) %reduce-scatter.2.cloned.1.call-update) | async-done | bytes 262160 | tf_op jit(solution)/shard_map/reduce_scatter | solution.py:38
  206.1 1.6 convert_bitcast_fusion
  207.7 5.4 %all-reduce.7 = bf16[16,4096]{1,0:T(8,128)(2,1)} all-reduce(f32[16,4096]{1,0:T(8,128)} %reduce-scatter.2.cloned.1.call-done), channel_id=1, replica_groups=mesh['head'=2,'seq'=8,'mp'=2] {'head'}, use_global_device_ids=true, to_apply=%region_4.5 | all-reduce | flops 65536 | bytes 393216 | tf_op jit(solution)/shard_map/psum | solution.py:46
  213.2 110.1 %all-reduce.6.cloned.1.call-done = f32[2304,4096]{1,0:T(8,128)} async-done(((f32[2304,4096]{1,0:T(8,128)}), f32[2304,4096]{1,0:T(8,128)}) %all-reduce.6.cloned.1.call-update) | async-done | bytes 37748752 | tf_op jit(solution)/shard_map/psum | solution.py:46
  323.3 27.3 %copy.19 = f32[2304,4096]{1,0:T(8,128)} copy(f32[2304,4096]{1,0:T(8,128)} %all-reduce.6.cloned.1.call-done) | data formatting | bytes 75497472
  (10 shorter events, 0.2 us)
Async XLA Ops:
  7.2 100.3 %all-reduce.4.cloned.1.call-start = ((), (), s32[]{:S(2)}) async-start(), calls=%async_computation.1 | async-start | bytes 2359296 | tf_op jit(solution)/shard_map/psum | solution.py:21
  8.2 8.8 %collective-permute-start = (bf16[16,4096]{1,0:T(8,128)(2,1)S(1)}, bf16[16,4096]{1,0:T(8,128)(2,1)S(1)}, u32[]{:S(2)}, u32[]{:S(2)}) collective-permute-start(bf16[16,4096]{1,0:T(8,128)(2,1)S(1)} %get-tuple-element.4), channel_id=1, source_target_pairs={{0,14},{2,0},{4,2},{6,4},{8,6},{10,8},{12,10},{14,12},{1,15},{3,1}... | collective-permute-start | bytes 393224 | tf_op jit(solution)/shard_map/ppermute | solution.py:16
  17.1 7.2 %collective-permute-start.1 = (bf16[32,4096]{1,0:T(8,128)(2,1)S(1)}, bf16[32,4096]{1,0:T(8,128)(2,1)S(1)}, u32[]{:S(2)}, u32[]{:S(2)}) collective-permute-start(bf16[32,4096]{1,0:T(8,128)(2,1)S(1)} %pad_maximum_fusion.1), channel_id=1, source_target_pairs={{0,12},{2,14},{4,0},{6,2},{8,4},{10,6},{12,8},{14,10},{1,13},{3,15... | collective-permute-start | bytes 786440 | tf_op jit(solution)/shard_map/ppermute | solution.py:16
  24.4 24.2 %collective-permute-start.2 = (bf16[64,4096]{1,0:T(8,128)(2,1)S(1)}, bf16[64,4096]{1,0:T(8,128)(2,1)S(1)}, u32[]{:S(2)}, u32[]{:S(2)}) collective-permute-start(bf16[64,4096]{1,0:T(8,128)(2,1)S(1)} %pad_maximum_fusion), channel_id=1, source_target_pairs={{0,8},{2,10},{4,12},{6,14},{8,0},{10,2},{12,4},{14,6},{1,9},{3,11}... | collective-permute-start | bytes 1572872 | tf_op jit(solution)/shard_map/ppermute | solution.py:16
  62.4 68.2 %copy-start.1 = (f32[1,128]{1,0:T(1,128)S(1)}, f32[1,128]{1,0:T(1,128)}, u32[]{:S(2)}) copy-start(f32[1,128]{1,0:T(1,128)} %param.9) | copy-start | bytes 1540
  62.4 68.2 %copy-start.2 = (s32[1,128]{1,0:T(1,128)S(1)}, s32[1,128]{1,0:T(1,128)}, u32[]{:S(2)}) copy-start(s32[1,128]{1,0:T(1,128)} %param.8) | copy-start | bytes 1540
  62.4 143.7 %reduce-scatter.2.cloned.1.call-start = ((), (), s32[]{:S(2)}) async-start(), calls=%async_computation.2 | async-start | bytes 2359296 | tf_op jit(solution)/shard_map/reduce_scatter | solution.py:38
  107.5 23.1 %copy-start = (f32[2304,128]{0,1:T(8,128)S(1)}, f32[2304,128]{0,1:T(8,128)}, u32[]{:S(2)}) copy-start(f32[2304,128]{0,1:T(8,128)} %all-reduce.4.cloned.1.call-done) | copy-start | bytes 3538948
  141.4 181.9 %all-reduce.6.cloned.1.call-start = ((), (), s32[]{:S(2)}) async-start(), calls=%async_computation.3 | async-start | bytes 75497472 | tf_op jit(solution)/shard_map/psum | solution.py:46
Sparse Core Ops, SparseCore 0:
  62.5 44.8 all-reduce.3
  141.5 64.5 reduce-scatter.1
  209.2 114.0 all-reduce.5
